TPU v7x, 32 devices: a whole 2x2x4 slice. The times are simulated.
32 devices in a mesh: node: 8 (over y, x, core), chip: 4 (over z).
Axes of the slice: x: 2, y: 2, z: 4, core: 2. Of those that a mesh axis runs over, the one named last changes fastest.
Arguments:
- momentum: float32 [32, 128, 512], P(('node', 'chip')), may hold values from -6 to 6
- gradient: bfloat16 [32, 128, 512], P(('node', 'chip')), may hold values from -6 to 6
- indices: int32 [32, 16, 32], P(('node', 'chip')), may hold values from 0 to 4095, as said below
Outputs:
- new_momentum: float32 [32, 128, 512], P(('node', 'chip'))
- update: float32 [128, 512], replicated
Inputs may be any that keep to these rules, and one draw needn't show every extreme that they name: `indices`: the 32 entries of each row name distinct coefficients of their span, coefficient (k, l) being k * 64 + l.
All inputs are finite; a program needn't handle non-finite values.
Results may differ from a plain program's by a relative error of at most 0.0029.
Values may be sent and summed in bfloat16 or wider, within the bound.
A program may use at most 64 MiB of HBM per device.

v0:
```python
import math
import jax
import jax.numpy as jnp
from jax import lax
from jax.sharding import PartitionSpec as P

SPAN = 64


def dct_table(edge_len):
    orders = jnp.arange(edge_len, dtype=jnp.float32)
    wave_no = orders[:, None]
    cell_no = orders[None, :]
    factor = jnp.where(wave_no == 0.0, math.sqrt(1.0 / edge_len), math.sqrt(2.0 / edge_len))
    return factor * jnp.cos(math.pi * (2.0 * cell_no + 1.0) * wave_no / (2.0 * edge_len))


def forward(grid_field, cosines, edge_len):
    row_blocks = grid_field.shape[0] // edge_len
    col_blocks = grid_field.shape[1] // edge_len
    blocks = grid_field.reshape(row_blocks, edge_len, col_blocks, edge_len).transpose(0, 2, 1, 3)
    coeffs = jnp.einsum(
        "kn,abnm,lm->abkl", cosines, blocks, cosines, precision=lax.Precision.HIGHEST
    )
    return coeffs.reshape(row_blocks * col_blocks, edge_len * edge_len)


def inverse_blocks(coeffs, cosines, edge_len):
    blocks = coeffs.reshape(coeffs.shape[0], edge_len, edge_len)
    return jnp.einsum("kn,ckl,lm->cnm", cosines, blocks, cosines, precision=lax.Precision.HIGHEST)


def place_blocks(blocks, row_count, col_count, edge_len):
    shaped = blocks.reshape(row_count // edge_len, col_count // edge_len, edge_len, edge_len)
    return shaped.transpose(0, 2, 1, 3).reshape(row_count, col_count)


def normalized(blocks):
    energy = jnp.mean(blocks * blocks, axis=(1, 2), keepdims=True)
    return blocks / jnp.sqrt(energy + 1.0)


def decode_block(picked, slots):
    n_spans = picked.shape[1]
    values_rows = jnp.moveaxis(picked, 1, 0).reshape(n_spans, -1)
    slot_rows = jnp.moveaxis(slots, 1, 0).reshape(n_spans, -1)
    orders = jnp.arange(SPAN, dtype=jnp.int32)[None, :]

    def one_span(pair):
        vals, where = pair
        wave_rows = (where // SPAN)[:, None] == orders
        wave_cols = (where % SPAN)[:, None] == orders
        left_hot = wave_rows.astype(jnp.bfloat16)
        right_hot = jnp.where(wave_cols, vals[:, None], jnp.zeros((), jnp.bfloat16))
        block = lax.dot_general(
            left_hot, right_hot, (((0,), (0,)), ((), ())), preferred_element_type=jnp.float32
        )
        return block.reshape(SPAN * SPAN)

    return lax.map(one_span, (values_rows, slot_rows))


def decode_lists(totals, picked, slots):
    count = picked.shape[0]
    group_len = 1
    for trial in range(1, 17):
        if count % trial == 0:
            group_len = trial
    picked_groups = picked.reshape((count // group_len, group_len) + picked.shape[1:])
    slot_groups = slots.reshape((count // group_len, group_len) + slots.shape[1:])

    def add_group(step, carry):
        return carry + decode_block(picked_groups[step], slot_groups[step])

    return lax.fori_loop(0, count // group_len, add_group, totals)


def shards(momentum, gradient, indices):
    cosines = dct_table(SPAN)
    row_count = momentum.shape[1]
    col_count = momentum.shape[2]
    blended = 0.9 * momentum[0] + gradient[0].astype(jnp.float32)
    coeffs = forward(blended, cosines, SPAN)
    slots = indices[0]
    picked = jnp.take_along_axis(coeffs, slots, axis=1).astype(jnp.bfloat16)
    sparse = decode_block(picked[None], indices)
    own_part = place_blocks(inverse_blocks(sparse, cosines, SPAN), row_count, col_count, SPAN)
    new_momentum = (blended - own_part)[None]
    partial_sum = decode_lists(
        jnp.zeros_like(coeffs),
        lax.all_gather(picked[None], "chip", axis=0, tiled=True),
        lax.all_gather(indices, "chip", axis=0, tiled=True),
    )
    totals = lax.psum(partial_sum, "node")
    update = place_blocks(
        normalized(inverse_blocks(totals, cosines, SPAN)), row_count, col_count, SPAN
    )
    return (new_momentum, update)


def solution(mesh):
    return jax.shard_map(
        shards,
        mesh=mesh,
        in_specs=(
            P(("node", "chip"), None, None),
            P(("node", "chip"), None, None),
            P(("node", "chip"), None, None),
        ),
        out_specs=(P(("node", "chip"), None, None), P()),
        check_vma=False,
    )
```

profile of v0, /device:TPU:0, one launch (start us, length us, event | category | flops | bytes accessed | tf_op | source)
XLA Modules:
  0.0 127.8 jit_solution(4356147614158876346)
XLA Ops:
  7.2 0.8 fusion.53
  8.0 14.8 %all_gather.6 = s32[4,16,32]{2,1,0:T(8,128)S(1)} all-gather(s32[1,16,32]{2,1,0:T(8,128)S(1)} %copy-done), channel_id=1, replica_groups=mesh['node'=8,'chip'=4] {'chip'}, dimensions={0}, use_global_device_ids=true | all-gather | bytes 10240 | tf_op jit(solution)/shard_map/all_gather | solution.py:92
  22.8 1.1 convert_add_fusion
  24.3 1.7 %fusion.20 = f32[2,8,64,64]{2,3,1,0:T(8,128)S(1)} fusion(f32[2,64,8,64]{1,3,2,0:T(8,128)S(1)} %copy.20, f32[64]{0:T(128)S(1)} %get-tuple-element.232, f32[64]{0:T(128)S(1)} %get-tuple-element.231), kind=kOutput, calls=%fused_computation.37 | convolution fusion | flops 50343936 | bytes 524800 | tf_op jit(solution)/shard_map/kn,abnm,lm->abkl/dot_general | solution.py:22
  26.0 0.7 fusion.22
  26.7 0.3 reshape.216
  27.0 4.8 %gather_fusion = bf16[512]{0:T(512)(128)(2,1)S(1)} fusion(bf16[16,4096]{1,0:T(8,128)(2,1)S(1)} %reshape.216, s32[512]{0:T(512)S(1)} %reshape.225), kind=kCustom, calls=%fused_computation | custom fusion | bytes 6144 | tf_op jit(solution)/shard_map/jit(take_along_axis)/gather | solution.py:85
  32.0 13.2 %all_gather.7 = bf16[4,16,32]{2,1,0:T(8,128)(2,1)S(1)} all-gather(bf16[1,16,32]{2,1,0:T(8,128)(2,1)S(1)} %select_convert_fusion), channel_id=1, replica_groups=mesh['node'=8,'chip'=4] {'chip'}, dimensions={0}, use_global_device_ids=true | all-gather | bytes 5120 | tf_op jit(solution)/shard_map/all_gather | solution.py:91
  45.4 13.3 %while.37 = (s32[]{:T(128)}, f32[16,4096]{1,0:T(8,128)S(1)}, s32[16,128]{1,0:T(8,128)S(1)}, bf16[16,128]{1,0:T(8,128)(2,1)S(1)}, s32[]{:T(128)}, /*index=5*/s32[]{:T(128)}) while((s32[]{:T(128)}, f32[16,4096]{1,0:T(8,128)S(1)}, s32[16,128]{1,0:T(8,128)S(1)}, bf16[16,128]{1,0:T(8,128)(2,1)S(1)}, s32[]{:T(128)}, ...), condition=%wide.region_3.4_spmd.clone.clone, body=%wide.region_2.3_spmd.clone.clone.sunk | while | flops 1075714 | bytes 86353 | solution.py:60
  45.5 0.3 fusion.72
  45.8 0.4 dynamic_update_slice.20
  46.3 0.3 fusion.72
  46.7 0.4 dynamic_update_slice.20
  47.1 0.3 fusion.72
  47.5 0.4 dynamic_update_slice.20
  48.0 0.3 fusion.72
  48.3 0.4 dynamic_update_slice.20
  48.8 0.3 fusion.72
  49.2 0.4 dynamic_update_slice.20
  49.6 0.3 fusion.72
  50.0 0.4 dynamic_update_slice.20
  50.8 0.4 dynamic_update_slice.20
  51.3 0.3 fusion.72
  51.7 0.4 dynamic_update_slice.20
  52.1 0.3 fusion.72
  52.5 0.4 dynamic_update_slice.20
  53.0 0.3 fusion.72
  53.3 0.4 dynamic_update_slice.20
  54.1 0.4 dynamic_update_slice.20
  54.6 0.3 fusion.72
  55.0 0.4 dynamic_update_slice.20
  55.5 0.3 fusion.72
  55.8 0.4 dynamic_update_slice.20
  56.3 0.3 fusion.72
  56.6 0.4 dynamic_update_slice.20
  57.5 0.4 dynamic_update_slice.20
  58.3 0.4 dynamic_update_slice.20
  58.9 1.0 copy.27
  60.1 13.3 %while.36 = (s32[]{:T(128)}, f32[16,4096]{1,0:T(8,128)S(1)}, s32[16,32]{1,0:T(8,128)S(1)}, bf16[16,32]{1,0:T(8,128)(2,1)S(1)}, s32[]{:T(128)}, /*index=5*/s32[]{:T(128)}) while((s32[]{:T(128)}, f32[16,4096]{1,0:T(8,128)S(1)}, s32[16,32]{1,0:T(8,128)S(1)}, bf16[16,32]{1,0:T(8,128)(2,1)S(1)}, s32[]{:T(128)}, ...), condition=%wide.region_1.2_spmd.clone.clone, body=%wide.region_0.1_spmd.clone.clone.sunk | while | flops 268930 | bytes 83089 | solution.py:60
  60.5 0.4 dynamic_update_slice.19
  61.3 0.4 dynamic_update_slice.19
  62.2 0.4 dynamic_update_slice.19
  63.0 0.4 dynamic_update_slice.19
  63.8 0.4 dynamic_update_slice.19
  64.7 0.4 dynamic_update_slice.19
  65.5 0.4 dynamic_update_slice.19
  66.3 0.4 dynamic_update_slice.19
  67.2 0.4 dynamic_update_slice.19
  68.0 0.4 dynamic_update_slice.19
  68.8 0.4 dynamic_update_slice.19
  69.7 0.4 dynamic_update_slice.19
  70.5 0.4 dynamic_update_slice.19
  71.3 0.4 dynamic_update_slice.19
  72.2 0.4 dynamic_update_slice.19
  73.0 0.4 dynamic_update_slice.19
  73.6 0.7 fusion.31
  74.4 0.7 fusion.29
  75.1 0.3 copy.24
  75.5 0.7 sub.16
  76.3 39.7 %all-reduce.2.cloned.1.call-done = f32[16,64,64]{1,2,0:T(8,128)} async-done(((f32[16,64,64]{1,2,0:T(8,128)}), f32[16,64,64]{1,2,0:T(8,128)}) %all-reduce.2.cloned.1.call-update) | async-done | bytes 262160 | tf_op jit(solution)/shard_map/psum | solution.py:94
  116.0 2.8 %fusion.27 = f32[16,64,64]{1,2,0:T(8,128)S(1)} fusion(f32[16,64,64]{1,2,0:T(8,128)} %all-reduce.2.cloned.1.call-done, f32[64]{0:T(128)S(1)} %get-tuple-element.232, f32[64]{0:T(128)S(1)} %get-tuple-element.231), kind=kOutput, calls=%fused_computation.47 | convolution fusion | flops 50343936 | bytes 524800 | tf_op jit(solution)/shard_map/kn,ckl,lm->cnm/dot_general | solution.py:30
  118.8 0.8 multiply_reduce_fusion
  119.7 0.3 copy.29
  120.1 0.9 reshape.224
  (171 shorter events, 10.9 us)
Async XLA Ops:
  7.2 108.9 %all-reduce.2.cloned.1.call-start = ((), (), s32[]{:S(2)}) async-start(), calls=%async_computation | async-start | bytes 1048576 | tf_op jit(solution)/shard_map/psum | solution.py:94
  7.2 0.8 copy-start
Sparse Core Ops, SparseCore 0:
  60.1 55.8 all-reduce.1
where the time goes:
time: 128 us
  waiting for transfers between devices  39.8 us (31%)
  blocking collectives  28 us (22%)
  local copies, waits for them, and re-layouts  24.9 us (19%)
  matrix products  15.8 us (12%)
  between operations  14.2 us (11%)
  other arithmetic  3.41 us (3%)
  loops' own time  1.61 us (1%)
    psum x1, waiting for transfers between devices, shards(): totals = lax.psum(partial_sum, 'node')  39.7 us
    all_gather x1, blocking collectives, shards(): lax.all_gather(indices, 'chip', axis=0, tiled=True)  14.8 us
    all_gather x1, blocking collectives, shards(): lax.all_gather(picked[None], 'chip', axis=0, tiled=True)  13.2 us
    dynamic_update_slice x32, local copies, waits for them, and re-layouts, decode_block(): return lax.map(one_span, (values_rows, slot_rows))  12.6 us
    dot_general x32, matrix products, one_span(): lax.dot_general(left_hot, right_hot, (((0,), (0,)), ((), ())), preferred_...  8.39 us
    gather x4, local copies, waits for them, and re-layouts, shards(): picked = jnp.take_along_axis(coeffs, slots, axis=1).astype(jnp.bfloat16)  5.09 us
    dot_general x4, matrix products, inverse_blocks(): jnp.einsum('kn,ckl,lm->cnm', cosines, blocks, cosines, precision=lax.Prec...  5.02 us
    broadcast_in_dim x32, local copies, waits for them, and re-layouts, decode_block(): return lax.map(one_span, (values_rows, slot_rows))  2.91 us
  transfers between devices with their start and end apart: 1, of which 1 were waited for; matrix products, arithmetic and copies ran while one was open for 12% of the time, Pallas kernels for 0%

commit v1 on v0

--- a/solution.py
+++ b/solution.py
@@ -91,7 +91,8 @@
         lax.all_gather(picked[None], "chip", axis=0, tiled=True),
         lax.all_gather(indices, "chip", axis=0, tiled=True),
     )
-    totals = lax.psum(partial_sum, "node")
+    terms = lax.all_gather(partial_sum, "node")
+    totals = jnp.sum(terms, axis=0)
     update = place_blocks(
         normalized(inverse_blocks(totals, cosines, SPAN)), row_count, col_count, SPAN
     )

time: 128 us -> 100 us (0.78)
  waiting for transfers between devices: 39.8 us -> 12.6 us
  matrix products: 15.8 us -> 13.8 us
  other arithmetic: 3.41 us -> 5.06 us
    psum x1 -> x0, waiting for transfers between devices: 39.7 us -> none  [shards(): totals = lax.psum(partial_sum, 'node')]
    all_gather x0 -> x1, waiting for transfers between devices: none -> 12.6 us  [shards(): terms = lax.all_gather(partial_sum, 'node')]
    dot_general x4, matrix products: 5.02 us -> 2.98 us  [inverse_blocks(): jnp.einsum('kn,ckl,lm->cnm', cosines, blocks, cosines, precision=lax.Prec...]
    reduce_sum x0 -> x1, other arithmetic: none -> 1.72 us  [shards(): totals = jnp.sum(terms, axis=0)]
  transfers between devices with their start and end apart: 1 -> 1, of which waited for: 1 -> 1; matrix products, arithmetic and copies ran while one was open for 12% -> 15% of each run, Pallas kernels for 0% -> 0%
where the time goes in v1:
time: 100 us
  blocking collectives  28.3 us (28%)
  local copies, waits for them, and re-layouts  24.6 us (25%)
  between operations  14.2 us (14%)
  matrix products  13.8 us (14%)
  waiting for transfers between devices  12.6 us (13%)
  other arithmetic  5.06 us (5%)
  loops' own time  1.61 us (2%)
    all_gather x1, blocking collectives, shards(): lax.all_gather(indices, 'chip', axis=0, tiled=True)  15 us
    all_gather x1, blocking collectives, shards(): lax.all_gather(picked[None], 'chip', axis=0, tiled=True)  13.2 us
    all_gather x1, waiting for transfers between devices, shards(): terms = lax.all_gather(partial_sum, 'node')  12.6 us
    dynamic_update_slice x32, local copies, waits for them, and re-layouts, decode_block(): return lax.map(one_span, (values_rows, slot_rows))  12.6 us
    dot_general x32, matrix products, one_span(): lax.dot_general(left_hot, right_hot, (((0,), (0,)), ((), ())), preferred_...  8.39 us
    gather x4, local copies, waits for them, and re-layouts, shards(): picked = jnp.take_along_axis(coeffs, slots, axis=1).astype(jnp.bfloat16)  5.09 us
    dot_general x4, matrix products, inverse_blocks(): jnp.einsum('kn,ckl,lm->cnm', cosines, blocks, cosines, precision=lax.Prec...  2.98 us
    broadcast_in_dim x32, local copies, waits for them, and re-layouts, decode_block(): return lax.map(one_span, (values_rows, slot_rows))  2.92 us
  transfers between devices with their start and end apart: 1, of which 1 were waited for; matrix products, arithmetic and copies ran while one was open for 15% of the time, Pallas kernels for 0%

profile of v1, /device:TPU:0, one launch (start us, length us, event | category | flops | bytes accessed | tf_op | source)
XLA Modules:
  0.0 100.2 jit_solution(13104030577230518320)
XLA Ops:
  7.2 0.7 fusion.53
  7.9 15.0 %all_gather.12 = s32[4,16,32]{2,1,0:T(8,128)S(1)} all-gather(s32[1,16,32]{2,1,0:T(8,128)} %param.9), channel_id=1, replica_groups=mesh['node'=8,'chip'=4] {'chip'}, dimensions={0}, use_global_device_ids=true | all-gather | bytes 10240 | tf_op jit(solution)/shard_map/all_gather | solution.py:92
  23.0 1.1 %convert_add_fusion = f32[1,128,512]{2,1,0:T(8,128)S(1)} fusion(bf16[1,128,512]{2,1,0:T(8,128)(2,1)} %param.8, f32[1,128,512]{2,1,0:T(8,128)} %param.7), kind=kLoop, calls=%fused_computation.41 | loop fusion | flops 196608 | bytes 655360 | tf_op jit(solution)/shard_map/add | solution.py:82
  24.4 1.7 %fusion.20 = f32[2,8,64,64]{2,3,1,0:T(8,128)S(1)} fusion(f32[2,64,8,64]{1,3,2,0:T(8,128)S(1)} %copy.20, f32[64]{0:T(128)S(1)} %get-tuple-element.232, f32[64]{0:T(128)S(1)} %get-tuple-element.231), kind=kOutput, calls=%fused_computation.37 | convolution fusion | flops 50343936 | bytes 524800 | tf_op jit(solution)/shard_map/kn,abnm,lm->abkl/dot_general | solution.py:22
  26.1 0.7 fusion.22
  26.8 0.3 reshape.216
  27.3 4.8 %gather_fusion = bf16[512]{0:T(512)(128)(2,1)S(1)} fusion(bf16[16,4096]{1,0:T(8,128)(2,1)S(1)} %reshape.216, s32[512]{0:T(512)S(1)} %reshape.225), kind=kCustom, calls=%fused_computation | custom fusion | bytes 6144 | tf_op jit(solution)/shard_map/jit(take_along_axis)/gather | solution.py:85
  32.2 13.2 %all_gather.13 = bf16[4,16,32]{2,1,0:T(8,128)(2,1)S(1)} all-gather(bf16[1,16,32]{2,1,0:T(8,128)(2,1)S(1)} %select_convert_fusion), channel_id=1, replica_groups=mesh['node'=8,'chip'=4] {'chip'}, dimensions={0}, use_global_device_ids=true | all-gather | bytes 5120 | tf_op jit(solution)/shard_map/all_gather | solution.py:91
  45.5 13.3 %while.37 = (s32[]{:T(128)}, f32[16,4096]{1,0:T(8,128)S(1)}, s32[16,128]{1,0:T(8,128)S(1)}, bf16[16,128]{1,0:T(8,128)(2,1)S(1)}, s32[]{:T(128)}, /*index=5*/s32[]{:T(128)}) while((s32[]{:T(128)}, f32[16,4096]{1,0:T(8,128)S(1)}, s32[16,128]{1,0:T(8,128)S(1)}, bf16[16,128]{1,0:T(8,128)(2,1)S(1)}, s32[]{:T(128)}, ...), condition=%wide.region_3.4_spmd.clone.clone, body=%wide.region_2.3_spmd.clone.clone.sunk | while | flops 1075714 | bytes 86361 | solution.py:60
  45.6 0.3 fusion.72
  46.0 0.4 dynamic_update_slice.20
  46.4 0.3 fusion.72
  46.8 0.4 dynamic_update_slice.20
  47.3 0.3 fusion.72
  47.6 0.4 dynamic_update_slice.20
  48.5 0.4 dynamic_update_slice.20
  48.9 0.3 fusion.72
  49.3 0.4 dynamic_update_slice.20
  49.8 0.3 fusion.72
  50.1 0.4 dynamic_update_slice.20
  50.6 0.3 fusion.72
  51.0 0.4 dynamic_update_slice.20
  51.4 0.3 fusion.72
  51.8 0.4 dynamic_update_slice.20
  52.3 0.3 fusion.72
  52.6 0.4 dynamic_update_slice.20
  53.1 0.3 fusion.72
  53.5 0.4 dynamic_update_slice.20
  53.9 0.3 fusion.72
  54.3 0.4 dynamic_update_slice.20
  54.8 0.3 fusion.72
  55.1 0.4 dynamic_update_slice.20
  56.0 0.4 dynamic_update_slice.20
  56.8 0.4 dynamic_update_slice.20
  57.6 0.4 dynamic_update_slice.20
  58.5 0.4 dynamic_update_slice.20
  58.9 0.7 copy-done
  59.7 13.3 %while.36 = (s32[]{:T(128)}, f32[16,4096]{1,0:T(8,128)S(1)}, s32[16,32]{1,0:T(8,128)S(1)}, bf16[16,32]{1,0:T(8,128)(2,1)S(1)}, s32[]{:T(128)}, /*index=5*/s32[]{:T(128)}) while((s32[]{:T(128)}, f32[16,4096]{1,0:T(8,128)S(1)}, s32[16,32]{1,0:T(8,128)S(1)}, bf16[16,32]{1,0:T(8,128)(2,1)S(1)}, s32[]{:T(128)}, ...), condition=%wide.region_1.2_spmd.clone.clone, body=%wide.region_0.1_spmd.clone.clone.sunk | while | flops 268930 | bytes 83097 | solution.py:60
  60.1 0.4 dynamic_update_slice.19
  61.0 0.4 dynamic_update_slice.19
  61.8 0.4 dynamic_update_slice.19
  62.6 0.4 dynamic_update_slice.19
  63.5 0.4 dynamic_update_slice.19
  64.3 0.4 dynamic_update_slice.19
  65.1 0.4 dynamic_update_slice.19
  66.0 0.4 dynamic_update_slice.19
  66.8 0.4 dynamic_update_slice.19
  67.6 0.4 dynamic_update_slice.19
  68.5 0.4 dynamic_update_slice.19
  69.3 0.4 dynamic_update_slice.19
  70.1 0.4 dynamic_update_slice.19
  71.0 0.4 dynamic_update_slice.19
  71.8 0.4 dynamic_update_slice.19
  72.6 0.4 dynamic_update_slice.19
  73.3 0.7 fusion.31
  74.0 0.7 fusion.29
  74.7 0.3 copy.24
  75.2 0.7 sub.16
  75.9 12.6 %all-gather.3.cloned.1.call-done = f32[128,4096]{1,0:T(8,128)} async-done(((f32[16,4096]{1,0:T(8,128)}), f32[128,4096]{1,0:T(8,128)}) %all-gather.3.cloned.1.call-update) | async-done | bytes 2097168 | tf_op jit(solution)/shard_map/all_gather | solution.py:94
  88.5 1.7 %reduce_sum.18 = f32[16,4096]{1,0:T(8,128)S(1)} reduce(f32[8,16,4096]{2,1,0:T(8,128)} %bitcast.83, f32[]{:T(128)} %constant.162.clone.1), dimensions={0}, to_apply=%region_4.5 | reduce | flops 458752 | bytes 2359300 | tf_op jit(solution)/shard_map/reduce_sum | solution.py:95
  90.5 0.7 fusion.27
  91.2 0.8 multiply_reduce_fusion
  92.2 0.3 copy.29
  92.5 0.9 reshape.224
  (173 shorter events, 11.2 us)
Async XLA Ops:
  7.2 81.4 %all-gather.3.cloned.1.call-start = ((), (), s32[]{:S(2)}) async-start(), calls=%async_computation | async-start | bytes 2359296 | tf_op jit(solution)/shard_map/all_gather | solution.py:94
  27.3 4.9 %copy-start.1 = (s32[1,16,32]{2,1,0:T(8,128)S(1)}, s32[1,16,32]{2,1,0:T(8,128)}, u32[]{:S(2)}) copy-start(s32[1,16,32]{2,1,0:T(8,128)} %param.9) | copy-start | bytes 6148
  58.9 0.7 copy-start
Sparse Core Ops, SparseCore 0:
  59.7 28.7 all-gather.2
